TPU v7x, 32 devices: a whole 2x2x4 slice. The times are simulated.
32 devices in a mesh: node: 8 (over z, core), local: 4 (over y, x).
Axes of the slice: x: 2, y: 2, z: 4, core: 2. Of those that a mesh axis runs over, the one named last changes fastest.
Arguments:
- tokens: bfloat16 [4096, 1280], P(('node', 'local')), may hold values from -64 to 64
- modality: int32 [4096], P(('node', 'local')), may hold values from 0 to 1, as said below
- expert_id: int32 [4096], P(('node', 'local')), may hold values from 0 to 31, as said below
- slot: int32 [4096], P(('node', 'local')), may hold values from 0 to 7, as said below
- type_embed: bfloat16 [2, 1280], replicated, may hold values from -6 to 6
- router: bfloat16 [1280, 32], replicated, may hold values from -1 to 1
- w_in: bfloat16 [32, 1280, 5120], P(('node', 'local')), may hold values from -0.15625 to 0.15625
- w_out: bfloat16 [32, 5120, 1280], P(('node', 'local')), may hold values from -0.078125 to 0.078125
Outputs:
- combined: bfloat16 [4096, 1280], P(('node', 'local'))
- losses: float32 [4], replicated
Inputs may be any that keep to these rules, and one draw needn't show every extreme that they name: `expert_id`: within each device's block of 128 tokens no expert is named more than 8 times, and in every draw some expert is named exactly 8 times in every block. `slot`: tokens of one device's block that name the same expert have distinct slots. `modality`: each device's block holds tokens of both modalities.
All inputs are finite; a program needn't handle non-finite values.
Results may differ from a plain program's by a relative error of at most 0.0095.
Values may be sent and summed in bfloat16 or wider, within the bound.
A program may use at most 64 MiB of HBM per device.

v0:
```python
import jax
import jax.numpy as jnp
from jax import lax
from jax.sharding import PartitionSpec as P

CAP = 8


def apply_expert(received, w_first, w_second):
    shape = received.shape
    flat = received.reshape(-1, shape[-1])
    hidden = jax.nn.gelu(
        jnp.dot(flat, w_first, preferred_element_type=jnp.float32), approximate=False
    ).astype(jnp.bfloat16)
    part = jnp.dot(hidden, w_second, preferred_element_type=jnp.float32).astype(jnp.bfloat16)
    return part.reshape(shape)


def local(tokens, modality, expert_id, slot, type_embed, router, w_in, w_out):
    width = tokens.shape[1]
    experts = router.shape[1]
    devices = lax.axis_size(("node", "local"))
    shards = devices // experts
    picked = jnp.where(
        modality[:, None] == 1,
        type_embed[1].astype(jnp.float32)[None, :],
        type_embed[0].astype(jnp.float32)[None, :],
    )
    mixed = (tokens.astype(jnp.float32) + picked).astype(jnp.bfloat16)
    logits = jnp.dot(mixed, router, preferred_element_type=jnp.float32)
    logp = jax.nn.log_softmax(logits, axis=-1)
    probs = jnp.exp(logp)
    entropy = -jnp.sum(probs * logp, axis=-1)
    chosen_mask = jnp.arange(experts, dtype=jnp.int32)[None, :] == expert_id[:, None]
    gate = jnp.sum(jnp.where(chosen_mask, probs, 0.0), axis=1)
    target = expert_id * CAP + slot
    select = (jnp.arange(experts * CAP, dtype=jnp.int32)[:, None] == target[None, :]).astype(
        jnp.bfloat16
    )
    buffer = jnp.dot(select, mixed, preferred_element_type=jnp.float32).astype(jnp.bfloat16)
    buffer = buffer.reshape(experts, 1, CAP, width)
    w_first = w_in[0]
    w_second = w_out[0]
    outgoing = jnp.broadcast_to(buffer, (experts, shards, CAP, width)).reshape(
        experts * shards, CAP, width
    )
    part = apply_expert(
        lax.all_to_all(outgoing, ("node", "local"), split_axis=0, concat_axis=0, tiled=True),
        w_first,
        w_second,
    )
    parts = lax.all_to_all(part, ("node", "local"), split_axis=0, concat_axis=0, tiled=True)
    totals = jnp.sum(
        parts.astype(jnp.float32).reshape(experts, shards, CAP, width), axis=1
    ).reshape(experts * CAP, width)
    gathered_rows = jnp.take(totals, target, axis=0)
    combined = (experts * gate[:, None] * gathered_rows).astype(jnp.bfloat16)
    member = jnp.stack([modality == 0, modality == 1], axis=1).astype(jnp.float32)
    counts = jnp.sum(member, axis=0)
    prob_sum = jnp.dot(member.T, probs, precision=lax.Precision.HIGHEST)
    entropy_sum = jnp.dot(member.T, entropy, precision=lax.Precision.HIGHEST)
    counts, prob_sum, entropy_sum = lax.psum((counts, prob_sum, entropy_sum), ("node", "local"))
    local_part = entropy_sum / counts
    mean_prob = prob_sum / counts[:, None]
    global_part = jnp.sum(mean_prob * jnp.log(mean_prob), axis=1)
    losses = jnp.concatenate([local_part, global_part])
    return (combined, losses)


def solution(mesh):
    placed = (
        P(("node", "local"), None),
        P(("node", "local")),
        P(("node", "local")),
        P(("node", "local")),
        P(),
        P(),
        P(("node", "local"), None, None),
        P(("node", "local"), None, None),
    )
    return jax.shard_map(
        local,
        mesh=mesh,
        in_specs=placed,
        out_specs=(P(("node", "local"), None), P()),
        check_vma=False,
    )
```

profile of v0, /device:TPU:1, one launch (start us, length us, event | category | flops | bytes accessed | tf_op | source)
XLA Modules:
  0.0 98.2 jit_solution(222852981420441175)
XLA Ops:
  0.6 0.0 copy-start
  0.6 0.7 compare_bitcast_fusion
  1.3 0.8 convert_reduce_fusion.1
  2.1 0.7 compare_and_fusion
  2.8 2.2 %fusion.50 = bf16[32,8,1280]{2,1,0:T(8,128)(2,1)} fusion(bf16[128,1280]{1,0:T(8,128)(2,1)} %param.8, f32[1280]{0:T(1024)S(1)} %get-tuple-element.5, f32[1280]{0:T(1024)S(1)} %get-tuple-element.4, pred[128]{0:T(512)(128)(4,1)S(1)} %get-tuple-element.13, s32[128]{0:T(128)S(1)} %get-tuple-element.10), kind=kOutput, calls=%fused_computation.56 | convolution fusion | flops 84901888 | bytes 993920 | tf_op jit(solution)/shard_map/dot_general | solution.py:40
  5.0 7.1 %all-to-all-start = ((bf16[32,8,1280]{2,1,0:T(8,128)(2,1)}), bf16[32,8,1280]{2,1,0:T(8,128)(2,1)S(1)}, u32[]{:S(2)}, u32[]{:S(2)}) async-start(bf16[32,8,1280]{2,1,0:T(8,128)(2,1)} %fusion.50), calls=%async_computation | async-start | bytes 1310720 | tf_op jit(solution)/shard_map/all_to_all | solution.py:48
  12.1 0.0 copy-done
  12.1 1.3 %fusion.103 = (f32[128]{0:T(128)S(1)}, f32[128,32]{0,1:T(8,128)S(1)}) fusion(bf16[1280,32]{0,1:T(8,128)(2,1)S(1)} %copy-done, bf16[128,1280]{1,0:T(8,128)(2,1)} %param.8, f32[1280]{0:T(1024)S(1)} %get-tuple-element.5, f32[1280]{0:T(1024)S(1)} %get-tuple-element.4, pred[128]{0:T(512)(128)(4,1)S(1)} %get-tuple-element.13), kind=kOutput, calls=%fused_computation.124 | convolution fusion | flops 11145088 | bytes 436864 | tf_op jit(solution)/shard_map/dot_general | solution.py:30
  13.4 0.0 copy-start.1
  13.5 16.4 %all-to-all-done = bf16[32,8,1280]{2,1,0:T(8,128)(2,1)S(1)} async-done(((bf16[32,8,1280]{2,1,0:T(8,128)(2,1)}), bf16[32,8,1280]{2,1,0:T(8,128)(2,1)S(1)}, u32[]{:S(2)}, u32[]{:S(2)}) %all-to-all-start) | async-done | bytes 655392 | tf_op jit(solution)/shard_map/all_to_all | solution.py:48
  29.9 21.6 %fusion.51 = bf16[32,8,1280]{2,1,0:T(8,128)(2,1)} fusion(bf16[1,5120,1280]{2,1,0:T(8,128)(2,1)} %param.15, bf16[1,1280,5120]{2,1,0:T(8,128)(2,1)} %param.14, bf16[32,8,1280]{2,1,0:T(8,128)(2,1)S(1)} %all-to-all-done), kind=kOutput, calls=%fused_computation.57 | convolution fusion | flops 6796410880 | bytes 27525120 | tf_op jit(solution)/shard_map/dot_general | solution.py:15
  51.5 3.7 %all-to-all-start.1 = ((bf16[32,8,1280]{2,1,0:T(8,128)(2,1)}), bf16[32,8,1280]{2,1,0:T(8,128)(2,1)S(1)}, u32[]{:S(2)}, u32[]{:S(2)}) async-start(bf16[32,8,1280]{2,1,0:T(8,128)(2,1)} %fusion.51), calls=%async_computation.1 | async-start | bytes 1310720 | tf_op jit(solution)/shard_map/all_to_all | solution.py:52
  55.2 0.1 convert_reduce_fusion.2
  55.3 0.0 copy-done.1
  55.3 0.1 convolution_bitcast_fusion
  55.5 0.1 fusion.64
  55.6 40.0 %all-reduce = (f32[2,32]{1,0:T(2,128)S(1)}, f32[2]{0:T(128)S(1)}, f32[2]{0:T(128)S(1)}) all-reduce(f32[2,32]{1,0:T(2,128)S(1)} %fusion.64, f32[2]{0:T(128)S(1)} %convert_reduce_fusion.2, f32[2]{0:T(128)S(1)} %convolution_bitcast_fusion), channel_id=1, replica_groups=mesh['node'=8,'local'=4] {'node','local'}, use_global_device_ids=true, to_apply=%region_7.8 | all-reduce | flops 68 | bytes 544 | tf_op jit(solution)/shard_map/psum | solution.py:62
  95.6 0.2 fusion.71
  95.8 0.6 pad_maximum_fusion
  96.4 0.0 all-to-all-done.1
  96.4 0.1 bitcast_convert_fusion
  96.5 0.9 gather_fusion
  97.4 0.9 multiply_convert_fusion
  (7 shorter events, 0.1 us)
Async XLA Ops:
  0.6 11.5 %copy-start = (bf16[1280,32]{0,1:T(8,128)(2,1)S(1)}, bf16[1280,32]{0,1:T(8,128)(2,1)}, u32[]{:S(2)}) copy-start(bf16[1280,32]{0,1:T(8,128)(2,1)} %param.13) | copy-start | bytes 245764
  5.0 24.8 %all-to-all-start = ((bf16[32,8,1280]{2,1,0:T(8,128)(2,1)}), bf16[32,8,1280]{2,1,0:T(8,128)(2,1)S(1)}, u32[]{:S(2)}, u32[]{:S(2)}) async-start(bf16[32,8,1280]{2,1,0:T(8,128)(2,1)} %fusion.50), calls=%async_computation | async-start | bytes 1310720 | tf_op jit(solution)/shard_map/all_to_all | solution.py:48
  13.4 41.9 %copy-start.1 = (s32[128]{0:T(128)S(1)}, s32[128]{0:T(128)}, u32[]{:S(2)}) copy-start(s32[128]{0:T(128)} %param.10) | copy-start | bytes 1540
  51.5 44.9 %all-to-all-start.1 = ((bf16[32,8,1280]{2,1,0:T(8,128)(2,1)}), bf16[32,8,1280]{2,1,0:T(8,128)(2,1)S(1)}, u32[]{:S(2)}, u32[]{:S(2)}) async-start(bf16[32,8,1280]{2,1,0:T(8,128)(2,1)} %fusion.51), calls=%async_computation.1 | async-start | bytes 1310720 | tf_op jit(solution)/shard_map/all_to_all | solution.py:52
where the time goes:
time: 100 us; the launch traced here: 98.2 us
  blocking collectives  40 us (40%)
  matrix products  25.3 us (25%)
  waiting for transfers between devices  16.4 us (16%)
  starting transfers between devices  10.7 us (11%)
  other arithmetic  4.1 us (4%)
    psum x1, blocking collectives, local(): lax.psum((counts, prob_sum, entropy_sum), ('node', 'local'))  40 us
    dot_general x1, matrix products, apply_expert(): jnp.dot(hidden, w_second, preferred_element_type=jnp.float32)  21.6 us
    all_to_all x1, waiting for transfers between devices, local(): lax.all_to_all(outgoing, ('node', 'local'), split_axis=0, concat_axis=0,...  16.4 us
    all_to_all x1, starting transfers between devices, local(): lax.all_to_all(outgoing, ('node', 'local'), split_axis=0, concat_axis=0,...  7.08 us
    all_to_all x1, starting transfers between devices, local(): lax.all_to_all(part, ('node', 'local'), split_axis=0, concat_axis=0, tile...  3.66 us
    dot_general x1, matrix products, local(): jnp.dot(select, mixed, preferred_element_type=jnp.float32)  2.22 us
  transfers between devices with their start and end apart: 2, of which 1 were waited for; matrix products, arithmetic and copies ran while one was open for 3% of the time, Pallas kernels for 0%

commit v1 on v0

v1 whole, which is shorter than its diff:
```python
import functools

import jax
import jax.numpy as jnp
from jax import lax
from jax.experimental import pallas as pl
from jax.experimental.pallas import tpu as pltpu
from jax.sharding import PartitionSpec as P

CAP = 8
LANES = 128
GROUPS = 2
MESH = pl.DeviceIdType.MESH


def tile_of(size, widest):
    tile = widest
    while size % tile:
        tile //= 2
    return tile


def gelu(x):
    half = 0.5 * x
    return half + half * lax.erf(x * 0.7071067811865476)


def column(row):
    size = row.shape[1]
    return jnp.transpose(jnp.broadcast_to(row, (size, size)))[:, :1]


def kernel(
    nodes, locals_, shards, experts, groups, hidden_tile, cols, weight_cuts,
    tok_hbm, ids_hbm, emb_hbm, router_hbm, w1_hbm, w2_hbm,
    out_ref, loss_ref,
    tok, ids, emb, router, w1, w2, stage, recv, hid, back, ret, stats, all_stats,
    in_sem, w1_sem, w2_sem, go_sem, got_sem, back_sem, ret_sem, stat_send, stat_recv,
):
    devices = nodes * locals_
    half = devices // groups
    width = tok.shape[1]
    count = tok.shape[0]
    chunks = width // cols
    me_n = lax.axis_index("node")
    me_l = lax.axis_index("local")
    me = me_n * locals_ + me_l
    my_pos = (me_n // groups) * locals_ + me_l

    def for_group(group, body):
        def step(i, _):
            peer_n = lax.rem(me_n + (i // locals_) * groups + group, nodes)
            peer_l = lax.rem(me_l + lax.rem(i, locals_), locals_)
            body(peer_n, peer_l)
            return 0

        lax.fori_loop(1 if group == 0 else 0, half, step, 0)

    def all_peers(body):
        for group in range(groups):
            for_group(group, body)

    barrier = pltpu.get_barrier_semaphore()
    all_peers(
        lambda n, l: pl.semaphore_signal(barrier, inc=1, device_id=(n, l), device_id_type=MESH)
    )
    loads = [
        pltpu.make_async_copy(src, dst, in_sem.at[i])
        for i, (src, dst) in enumerate(
            ((ids_hbm, ids), (emb_hbm, emb), (tok_hbm, tok), (router_hbm, router))
        )
    ]
    for load in loads:
        load.start()
    weight_loads = []
    for hbm, vmem, sem in ((w1_hbm, w1, w1_sem), (w2_hbm, w2, w2_sem)):
        rows = vmem.shape[0] // weight_cuts
        weight_loads.append(
            [
                pltpu.make_async_copy(
                    hbm.at[0, pl.ds(i * rows, rows)], vmem.at[pl.ds(i * rows, rows)], sem.at[i]
                )
                for i in range(weight_cuts)
            ]
        )
        for load in weight_loads[-1]:
            load.start()
    for load in loads:
        load.wait()

    modality = ids[0:1, :]
    expert_id = ids[1:2, :]
    slot = ids[2:3, :]
    is_text = column(modality) == 1
    picked = jnp.where(
        is_text, emb[1:2, :].astype(jnp.float32), emb[0:1, :].astype(jnp.float32)
    )
    mixed = (tok[...].astype(jnp.float32) + picked).astype(jnp.bfloat16)
    place = lax.broadcasted_iota(jnp.int32, (experts * CAP, count), 0)
    select = (place == expert_id * CAP + slot).astype(jnp.bfloat16)
    stage[...] = (
        jnp.dot(select, mixed, preferred_element_type=jnp.float32)
        .reshape(experts, CAP, width)
        .astype(jnp.bfloat16)
    )

    pl.semaphore_wait(barrier, devices - 1)

    for group in range(groups):
        if group == 0:
            pltpu.make_async_copy(
                stage.at[me // shards], recv.at[0, my_pos], got_sem.at[0]
            ).start()

        def dispatch(n, l):
            pltpu.make_async_remote_copy(
                src_ref=stage.at[(n * locals_ + l) // shards],
                dst_ref=recv.at[group, my_pos],
                send_sem=go_sem.at[group],
                recv_sem=got_sem.at[group],
                device_id=(n, l),
                device_id_type=MESH,
            ).start()

        for_group(group, dispatch)

    logits = jnp.dot(mixed, router[...], preferred_element_type=jnp.float32)
    shifted = logits - jnp.max(logits, axis=-1, keepdims=True)
    logp = shifted - jnp.log(jnp.sum(jnp.exp(shifted), axis=-1, keepdims=True))
    probs = jnp.exp(logp)
    entropy = -jnp.sum(probs * logp, axis=-1, keepdims=True)
    expert_col = column(expert_id)
    lane = lax.broadcasted_iota(jnp.int32, (count, experts), 1)
    gate = jnp.sum(jnp.where(lane == expert_col, probs, 0.0), axis=1, keepdims=True)
    stats[...] = jnp.zeros_like(stats)
    for m in range(2):
        member = is_text if m == 1 else jnp.logical_not(is_text)
        stats[m : m + 1, 0:experts] = jnp.sum(
            jnp.where(member, probs, 0.0), axis=0, keepdims=True
        )
        stats[m : m + 1, experts : experts + 1] = jnp.sum(
            jnp.where(member, entropy, 0.0), axis=0, keepdims=True
        )
        stats[m : m + 1, experts + 1 : experts + 2] = jnp.sum(
            jnp.where(member, 1.0, 0.0), axis=0, keepdims=True
        )
    scale = experts * gate
    spot = lax.broadcasted_iota(jnp.int32, (count, devices * CAP), 1)
    first = expert_col * (shards * CAP) + column(slot)
    found = spot == first
    for s in range(1, shards):
        found = jnp.logical_or(found, spot == first + s * CAP)
    pick = found.astype(jnp.bfloat16)

    pltpu.make_async_copy(stats, all_stats.at[me], stat_recv).start()
    all_peers(
        lambda n, l: pltpu.make_async_remote_copy(
            src_ref=stats,
            dst_ref=all_stats.at[me],
            send_sem=stat_send,
            recv_sem=stat_recv,
            device_id=(n, l),
            device_id_type=MESH,
        ).start()
    )

    for group in range(groups):
        pltpu.make_async_copy(recv.at[group], recv.at[group], got_sem.at[group]).wait()
        rows = recv[group].astype(jnp.float32).reshape(half * CAP, width).astype(jnp.bfloat16)
        if group == 0:
            for load in weight_loads[0]:
                load.wait()

        def first_layer(i, _):
            at = pl.ds(pl.multiple_of(i * hidden_tile, hidden_tile), hidden_tile)
            hid[:, at] = gelu(
                jnp.dot(rows, w1[:, at], preferred_element_type=jnp.float32)
            ).astype(jnp.bfloat16)
            return 0

        lax.fori_loop(0, hid.shape[1] // hidden_tile, first_layer, 0)
        if group == 0:
            for load in weight_loads[1]:
                load.wait()

        def second_layer(c, _):
            at = pl.ds(pl.multiple_of(c * cols, cols), cols)
            back[group, c] = (
                jnp.dot(hid[...], w2[:, at], preferred_element_type=jnp.float32)
                .reshape(half, CAP, cols)
                .astype(jnp.bfloat16)
            )
            if group == 0:
                pltpu.make_async_copy(
                    back.at[0, c, my_pos], ret.at[c, me], ret_sem.at[0, c]
                ).start()

            def give(n, l):
                pltpu.make_async_remote_copy(
                    src_ref=back.at[group, c, (n // groups) * locals_ + l],
                    dst_ref=ret.at[c, me],
                    send_sem=back_sem.at[group, c],
                    recv_sem=ret_sem.at[group, c],
                    device_id=(n, l),
                    device_id_type=MESH,
                ).start()

            for_group(group, give)
            return 0

        lax.fori_loop(0, chunks, second_layer, 0)

    pltpu.make_async_copy(all_stats, all_stats, stat_recv).wait()
    total = jnp.sum(all_stats[...], axis=0)
    tokens_of = total[:, experts + 1 : experts + 2]
    entropy_mean = total[:, experts : experts + 1] / tokens_of
    mean = total[:, 0:experts] / tokens_of
    spread = jnp.sum(mean * jnp.log(mean), axis=1, keepdims=True)
    loss_ref[0] = entropy_mean[0, 0]
    loss_ref[1] = entropy_mean[1, 0]
    loss_ref[2] = spread[0, 0]
    loss_ref[3] = spread[1, 0]

    for c in range(chunks):
        for group in range(groups):
            part = ret.at[c, pl.ds(0, half)]
            pltpu.make_async_copy(part, part, ret_sem.at[group, c]).wait()
        table = (
            ret[c].astype(jnp.float32).reshape(devices * CAP, cols).astype(jnp.bfloat16)
        )
        out_ref[:, c * cols : (c + 1) * cols] = (
            scale * jnp.dot(pick, table, preferred_element_type=jnp.float32)
        ).astype(jnp.bfloat16)

    for group in range(groups):
        sent = half - 1 if group == 0 else half
        done = recv.at[group, pl.ds(0, sent)]
        pltpu.make_async_copy(done, done, go_sem.at[group]).wait()
        for c in range(chunks):
            done = back.at[group, c, pl.ds(0, sent)]
            pltpu.make_async_copy(done, done, back_sem.at[group, c]).wait()
    done = all_stats.at[pl.ds(0, devices - 1)]
    pltpu.make_async_copy(done, done, stat_send).wait()


def local(nodes, locals_, tokens, modality, expert_id, slot, type_embed, router, w_in, w_out):
    count, width = tokens.shape
    experts = router.shape[1]
    devices = nodes * locals_
    shards = devices // experts
    hidden = w_in.shape[2]
    groups = GROUPS if nodes % GROUPS == 0 else 1
    half = devices // groups
    cols = tile_of(width, 256)
    chunks = width // cols
    cuts = 5 if width % 80 == 0 and hidden % 80 == 0 else 1
    ids = jnp.stack([modality, expert_id, slot])
    bf16 = jnp.bfloat16
    any_space = pl.BlockSpec(memory_space=pl.ANY)
    dma = pltpu.SemaphoreType.DMA
    combined, losses = pl.pallas_call(
        functools.partial(
            kernel, nodes, locals_, shards, experts, groups, tile_of(hidden, 512), cols, cuts
        ),
        out_shape=(
            jax.ShapeDtypeStruct((count, width), bf16),
            jax.ShapeDtypeStruct((4,), jnp.float32),
        ),
        in_specs=[any_space] * 6,
        out_specs=(
            pl.BlockSpec(memory_space=pltpu.VMEM),
            pl.BlockSpec(memory_space=pltpu.SMEM),
        ),
        scratch_shapes=[
            pltpu.VMEM((count, width), bf16),
            pltpu.VMEM((3, count), jnp.int32),
            pltpu.VMEM((2, width), bf16),
            pltpu.VMEM((width, experts), bf16),
            pltpu.VMEM((width, hidden), bf16),
            pltpu.VMEM((hidden, width), bf16),
            pltpu.VMEM((experts, CAP, width), bf16),
            pltpu.VMEM((groups, half, CAP, width), bf16),
            pltpu.VMEM((half * CAP, hidden), bf16),
            pltpu.VMEM((groups, chunks, half, CAP, cols), bf16),
            pltpu.VMEM((chunks, devices, CAP, cols), bf16),
            pltpu.VMEM((2, LANES), jnp.float32),
            pltpu.VMEM((devices, 2, LANES), jnp.float32),
            dma((4,)),
            dma((cuts,)),
            dma((cuts,)),
            dma((groups,)),
            dma((groups,)),
            dma((groups, chunks)),
            dma((groups, chunks)),
            dma,
            dma,
        ],
        compiler_params=pltpu.CompilerParams(
            collective_id=0, has_side_effects=True, vmem_limit_bytes=62 * 1024 * 1024
        ),
    )(tokens, ids, type_embed, router, w_in, w_out)
    return combined, losses


def solution(mesh):
    placed = (
        P(("node", "local"), None),
        P(("node", "local")),
        P(("node", "local")),
        P(("node", "local")),
        P(),
        P(),
        P(("node", "local"), None, None),
        P(("node", "local"), None, None),
    )
    return jax.shard_map(
        functools.partial(local, mesh.shape["node"], mesh.shape["local"]),
        mesh=mesh,
        in_specs=placed,
        out_specs=(P(("node", "local"), None), P()),
        check_vma=False,
    )
```

time: 100 us -> 54.9 us (0.55); the launches traced: 98.2 us -> 54.7 us
  Pallas kernels: 0 us -> 48.1 us
  blocking collectives: 40 us -> 0 us
  matrix products: 25.3 us -> 0 us
  waiting for transfers between devices: 16.4 us -> 0 us
  starting transfers between devices: 10.7 us -> 0 us
  local copies, waits for them, and re-layouts: 0.9 us -> 4.62 us
  other arithmetic: 4.1 us -> 1.29 us
    pallas_call x0 -> x1, Pallas kernels: none -> 48.1 us  [local(): pl.pallas_call(functools.partial(kernel, nodes, locals_, shards, experts,...]
    psum x1 -> x0, blocking collectives: 40 us -> none  [local(): lax.psum((counts, prob_sum, entropy_sum), ('node', 'local'))]
    dot_general x5 -> x0, matrix products: 25.3 us -> none  [the longest x1 21.6 us: apply_expert(): jnp.dot(hidden, w_second, preferred_element_type=jnp.float32)]
    all_to_all x2 -> x0, waiting for transfers between devices: 16.4 us -> none  [the longest x1 16.4 us: local(): lax.all_to_all(outgoing, ('node', 'local'), split_axis=0, concat_axis=0,...]
    all_to_all x2 -> x0, starting transfers between devices: 10.7 us -> none  [the longest x1 7.08 us: local(): lax.all_to_all(outgoing, ('node', 'local'), split_axis=0, concat_axis=0,...]
    unnamed x4 -> x3, local copies, waits for them, and re-layouts: 0.02 us -> 4.62 us
  transfers between devices with their start and end apart: 2 -> 0, of which waited for: 1 -> 0; matrix products, arithmetic and copies ran while one was open for 3% -> 0% of each run, Pallas kernels for 0% -> 0%
where the time goes in v1:
time: 54.9 us; the launch traced here: 54.7 us
  Pallas kernels  48.1 us (88%)
  local copies, waits for them, and re-layouts  4.62 us (8%)
  other arithmetic  1.29 us (2%)
  between operations  0.64 us (1%)
    pallas_call x1, Pallas kernels, local(): pl.pallas_call(functools.partial(kernel, nodes, locals_, shards, experts,...  48.1 us
    unnamed x3, local copies, waits for them, and re-layouts  4.62 us
    another operation x1, other arithmetic, local(): ids = jnp.stack([modality, expert_id, slot])  1.29 us

profile of v1, /device:TPU:1, one launch (start us, length us, event | category | flops | bytes accessed | tf_op | source)
XLA Modules:
  0.0 54.7 jit_solution(10634593202185891933)
XLA Ops:
  0.6 1.3 %pad_add_fusion.ids_hbm = s32[3,128]{1,0:T(4,128)} fusion(s32[1,128]{1,0:T(1,128)} %bitcast.3, s32[1,128]{1,0:T(1,128)} %bitcast.4, s32[1,128]{1,0:T(1,128)} %bitcast.5), kind=kLoop, calls=%fused_computation | loop fusion | flops 768 | bytes 3072 | tf_op jit(solution)/shard_map/stack | solution.py:257
  1.9 1.8 %copy.10.router_hbm = bf16[1280,32]{1,0:T(8,128)(2,1)} copy(bf16[1280,32]{0,1:T(8,128)(2,1)} %param.13) | data formatting | bytes 163840 | tf_op args[5]
  3.7 48.1 %shard_map.95 = (bf16[128,1280]{1,0:T(8,128)(2,1)}, f32[4]{0:T(128)}) custom-call(bf16[128,1280]{1,0:T(8,128)(2,1)} %tok_hbm.1, s32[3,128]{1,0:T(4,128)} %pad_add_fusion.ids_hbm, bf16[2,1280]{1,0:T(2,128)(2,1)} %emb_hbm.1, bf16[1280,32]{1,0:T(8,128)(2,1)} %copy.10.router_hbm, bf16[1,1280,5120]{2,1,0:T(8,128)(2,1)} %w1_hbm.1, bf16[1,5120,1280]{2,1,0:T(8,128)(2,1)} %w2_hbm.1), custom_call_target="tpu_custom_call" | custom-call | tf_op jit(solution)/shard_map/pallas_call | solution.py:261
  51.8 1.7 %copy.13 = bf16[128,1280]{1,0:T(8,128)(2,1)} copy(bf16[128,1280]{1,0:T(8,128)(2,1)} %get-tuple-element.4) | data formatting | bytes 655360
  53.5 1.1 %copy.14 = f32[4]{0:T(128)} copy(f32[4]{0:T(128)} %get-tuple-element.5) | data formatting | bytes 32

commit v2 on v1

--- a/solution.py
+++ b/solution.py
@@ -32,9 +32,9 @@
 
 def kernel(
     nodes, locals_, shards, experts, groups, hidden_tile, cols, weight_cuts,
-    tok_hbm, ids_hbm, emb_hbm, router_hbm, w1_hbm, w2_hbm,
-    out_ref, loss_ref,
-    tok, ids, emb, router, w1, w2, stage, recv, hid, back, ret, stats, all_stats,
+    tok_hbm, mod_hbm, eid_hbm, slot_hbm, emb_hbm, router_hbm, w1_hbm, w2_hbm,
+    ret, pick, scale, all_stats,
+    tok, mod, eid, slots, emb, router, w1, w2, stage, recv, hid, back, stats, row_stats, row_sum,
     in_sem, w1_sem, w2_sem, go_sem, got_sem, back_sem, ret_sem, stat_send, stat_recv,
 ):
     devices = nodes * locals_
@@ -67,7 +67,14 @@
     loads = [
         pltpu.make_async_copy(src, dst, in_sem.at[i])
         for i, (src, dst) in enumerate(
-            ((ids_hbm, ids), (emb_hbm, emb), (tok_hbm, tok), (router_hbm, router))
+            (
+                (tok_hbm, tok),
+                (mod_hbm, mod),
+                (eid_hbm, eid),
+                (slot_hbm, slots),
+                (emb_hbm, emb),
+                (router_hbm, router),
+            )
         )
     ]
     for load in loads:
@@ -83,14 +90,12 @@
                 for i in range(weight_cuts)
             ]
         )
-        for load in weight_loads[-1]:
-            load.start()
     for load in loads:
         load.wait()
 
-    modality = ids[0:1, :]
-    expert_id = ids[1:2, :]
-    slot = ids[2:3, :]
+    modality = mod[...]
+    expert_id = eid[...]
+    slot = slots[...]
     is_text = column(modality) == 1
     picked = jnp.where(
         is_text, emb[1:2, :].astype(jnp.float32), emb[0:1, :].astype(jnp.float32)
@@ -124,7 +129,13 @@
 
         for_group(group, dispatch)
 
-    logits = jnp.dot(mixed, router[...], preferred_element_type=jnp.float32)
+    for weight_load in weight_loads:
+        for load in weight_load:
+            load.start()
+
+    logits = lax.dot_general(
+        mixed, router[...], (((1,), (1,)), ((), ())), preferred_element_type=jnp.float32
+    )
     shifted = logits - jnp.max(logits, axis=-1, keepdims=True)
     logp = shifted - jnp.log(jnp.sum(jnp.exp(shifted), axis=-1, keepdims=True))
     probs = jnp.exp(logp)
@@ -144,25 +155,28 @@
         stats[m : m + 1, experts + 1 : experts + 2] = jnp.sum(
             jnp.where(member, 1.0, 0.0), axis=0, keepdims=True
         )
-    scale = experts * gate
+    scale[...] = experts * gate
     spot = lax.broadcasted_iota(jnp.int32, (count, devices * CAP), 1)
     first = expert_col * (shards * CAP) + column(slot)
     found = spot == first
     for s in range(1, shards):
         found = jnp.logical_or(found, spot == first + s * CAP)
-    pick = found.astype(jnp.bfloat16)
-
-    pltpu.make_async_copy(stats, all_stats.at[me], stat_recv).start()
-    all_peers(
-        lambda n, l: pltpu.make_async_remote_copy(
+    pick[...] = found.astype(jnp.bfloat16)
+
+    pltpu.make_async_copy(stats, row_stats.at[me_l], stat_recv.at[0]).start()
+
+    def share_row(i, _):
+        pltpu.make_async_remote_copy(
             src_ref=stats,
-            dst_ref=all_stats.at[me],
-            send_sem=stat_send,
-            recv_sem=stat_recv,
-            device_id=(n, l),
+            dst_ref=row_stats.at[me_l],
+            send_sem=stat_send.at[0],
+            recv_sem=stat_recv.at[0],
+            device_id=(me_n, lax.rem(me_l + i, locals_)),
             device_id_type=MESH,
         ).start()
-    )
+        return 0
+
+    lax.fori_loop(1, locals_, share_row, 0)
 
     for group in range(groups):
         pltpu.make_async_copy(recv.at[group], recv.at[group], got_sem.at[group]).wait()
@@ -180,6 +194,8 @@
 
         lax.fori_loop(0, hid.shape[1] // hidden_tile, first_layer, 0)
         if group == 0:
+            pltpu.make_async_copy(row_stats, row_stats, stat_recv.at[0]).wait()
+            row_sum[...] = jnp.sum(row_stats[...], axis=0)
             for load in weight_loads[1]:
                 load.wait()
 
@@ -209,8 +225,50 @@
             return 0
 
         lax.fori_loop(0, chunks, second_layer, 0)
-
-    pltpu.make_async_copy(all_stats, all_stats, stat_recv).wait()
+        if group == 0:
+            pltpu.make_async_copy(row_sum, all_stats.at[me_n], stat_recv.at[1]).start()
+
+            def share_sum(i, _):
+                pltpu.make_async_remote_copy(
+                    src_ref=row_sum,
+                    dst_ref=all_stats.at[me_n],
+                    send_sem=stat_send.at[1],
+                    recv_sem=stat_recv.at[1],
+                    device_id=(lax.rem(me_n + i, nodes), me_l),
+                    device_id_type=MESH,
+                ).start()
+                return 0
+
+            lax.fori_loop(1, nodes, share_sum, 0)
+
+    pltpu.make_async_copy(all_stats, all_stats, stat_recv.at[1]).wait()
+    for c in range(chunks):
+        for group in range(groups):
+            part = ret.at[c, pl.ds(0, half)]
+            pltpu.make_async_copy(part, part, ret_sem.at[group, c]).wait()
+
+    for group in range(groups):
+        sent = half - 1 if group == 0 else half
+        done = recv.at[group, pl.ds(0, sent)]
+        pltpu.make_async_copy(done, done, go_sem.at[group]).wait()
+        for c in range(chunks):
+            done = back.at[group, c, pl.ds(0, sent)]
+            pltpu.make_async_copy(done, done, back_sem.at[group, c]).wait()
+    for i, done in enumerate(
+        (row_stats.at[pl.ds(0, locals_ - 1)], all_stats.at[pl.ds(0, nodes - 1)])
+    ):
+        pltpu.make_async_copy(done, done, stat_send.at[i]).wait()
+
+
+def finish(experts, ret, pick, scale, all_stats, out_ref, loss_ref):
+    chunks, devices, _, cols = ret.shape
+    for c in range(chunks):
+        table = (
+            ret[c].astype(jnp.float32).reshape(devices * CAP, cols).astype(jnp.bfloat16)
+        )
+        out_ref[:, c * cols : (c + 1) * cols] = (
+            scale[...] * jnp.dot(pick[...], table, preferred_element_type=jnp.float32)
+        ).astype(jnp.bfloat16)
     total = jnp.sum(all_stats[...], axis=0)
     tokens_of = total[:, experts + 1 : experts + 2]
     entropy_mean = total[:, experts : experts + 1] / tokens_of
@@ -221,27 +279,6 @@
     loss_ref[2] = spread[0, 0]
     loss_ref[3] = spread[1, 0]
 
-    for c in range(chunks):
-        for group in range(groups):
-            part = ret.at[c, pl.ds(0, half)]
-            pltpu.make_async_copy(part, part, ret_sem.at[group, c]).wait()
-        table = (
-            ret[c].astype(jnp.float32).reshape(devices * CAP, cols).astype(jnp.bfloat16)
-        )
-        out_ref[:, c * cols : (c + 1) * cols] = (
-            scale * jnp.dot(pick, table, preferred_element_type=jnp.float32)
-        ).astype(jnp.bfloat16)
-
-    for group in range(groups):
-        sent = half - 1 if group == 0 else half
-        done = recv.at[group, pl.ds(0, sent)]
-        pltpu.make_async_copy(done, done, go_sem.at[group]).wait()
-        for c in range(chunks):
-            done = back.at[group, c, pl.ds(0, sent)]
-            pltpu.make_async_copy(done, done, back_sem.at[group, c]).wait()
-    done = all_stats.at[pl.ds(0, devices - 1)]
-    pltpu.make_async_copy(done, done, stat_send).wait()
-
 
 def local(nodes, locals_, tokens, modality, expert_id, slot, type_embed, router, w_in, w_out):
     count, width = tokens.shape
@@ -251,55 +288,73 @@
     hidden = w_in.shape[2]
     groups = GROUPS if nodes % GROUPS == 0 else 1
     half = devices // groups
-    cols = tile_of(width, 256)
+    cols = width // 2 if width % 256 == 0 else width
     chunks = width // cols
     cuts = 5 if width % 80 == 0 and hidden % 80 == 0 else 1
-    ids = jnp.stack([modality, expert_id, slot])
     bf16 = jnp.bfloat16
+    vmem_space = pl.BlockSpec(memory_space=pltpu.VMEM)
     any_space = pl.BlockSpec(memory_space=pl.ANY)
     dma = pltpu.SemaphoreType.DMA
-    combined, losses = pl.pallas_call(
+    held = pl.pallas_call(
         functools.partial(
             kernel, nodes, locals_, shards, experts, groups, tile_of(hidden, 512), cols, cuts
         ),
         out_shape=(
-            jax.ShapeDtypeStruct((count, width), bf16),
-            jax.ShapeDtypeStruct((4,), jnp.float32),
+            jax.ShapeDtypeStruct((chunks, devices, CAP, cols), bf16),
+            jax.ShapeDtypeStruct((count, devices * CAP), bf16),
+            jax.ShapeDtypeStruct((count, 1), jnp.float32),
+            jax.ShapeDtypeStruct((nodes, 2, LANES), jnp.float32),
         ),
-        in_specs=[any_space] * 6,
-        out_specs=(
-            pl.BlockSpec(memory_space=pltpu.VMEM),
-            pl.BlockSpec(memory_space=pltpu.SMEM),
-        ),
+        in_specs=[any_space] * 8,
+        out_specs=(vmem_space,) * 4,
         scratch_shapes=[
             pltpu.VMEM((count, width), bf16),
-            pltpu.VMEM((3, count), jnp.int32),
+            pltpu.VMEM((1, count), jnp.int32),
+            pltpu.VMEM((1, count), jnp.int32),
+            pltpu.VMEM((1, count), jnp.int32),
             pltpu.VMEM((2, width), bf16),
-            pltpu.VMEM((width, experts), bf16),
+            pltpu.VMEM((experts, width), bf16),
             pltpu.VMEM((width, hidden), bf16),
             pltpu.VMEM((hidden, width), bf16),
             pltpu.VMEM((experts, CAP, width), bf16),
             pltpu.VMEM((groups, half, CAP, width), bf16),
             pltpu.VMEM((half * CAP, hidden), bf16),
             pltpu.VMEM((groups, chunks, half, CAP, cols), bf16),
-            pltpu.VMEM((chunks, devices, CAP, cols), bf16),
             pltpu.VMEM((2, LANES), jnp.float32),
-            pltpu.VMEM((devices, 2, LANES), jnp.float32),
-            dma((4,)),
+            pltpu.VMEM((locals_, 2, LANES), jnp.float32),
+            pltpu.VMEM((2, LANES), jnp.float32),
+            dma((6,)),
             dma((cuts,)),
             dma((cuts,)),
             dma((groups,)),
             dma((groups,)),
             dma((groups, chunks)),
             dma((groups, chunks)),
-            dma,
-            dma,
+            dma((2,)),
+            dma((2,)),
         ],
         compiler_params=pltpu.CompilerParams(
             collective_id=0, has_side_effects=True, vmem_limit_bytes=62 * 1024 * 1024
         ),
-    )(tokens, ids, type_embed, router, w_in, w_out)
-    return combined, losses
+    )(
+        tokens,
+        modality.reshape(1, count),
+        expert_id.reshape(1, count),
+        slot.reshape(1, count),
+        type_embed,
+        router.T,
+        w_in,
+        w_out,
+    )
+    return pl.pallas_call(
+        functools.partial(finish, experts),
+        out_shape=(
+            jax.ShapeDtypeStruct((count, width), bf16),
+            jax.ShapeDtypeStruct((4,), jnp.float32),
+        ),
+        in_specs=[vmem_space] * 4,
+        out_specs=(vmem_space, pl.BlockSpec(memory_space=pltpu.SMEM)),
+    )(*held)
 
 
 def solution(mesh):

time: 54.9 us -> 41.4 us (0.75)
  Pallas kernels: 48.1 us -> 40.6 us
  local copies, waits for them, and re-layouts: 4.62 us -> 0 us
  other arithmetic: 1.29 us -> 0 us
    pallas_call x1, Pallas kernels: 48.1 us -> 38.4 us  [local(): pl.pallas_call(functools.partial(kernel, nodes, locals_, shards, experts,...]
    unnamed x3 -> x0, local copies, waits for them, and re-layouts: 4.62 us -> none
    pallas_call x0 -> x1, Pallas kernels: none -> 2.15 us  [local(): pl.pallas_call(functools.partial(finish, experts), out_shape=(jax.ShapeDt...]
    another operation x1 -> x0, other arithmetic: 1.29 us -> none  [local(): ids = jnp.stack([modality, expert_id, slot])]
where the time goes in v2:
time: 41.4 us; the launch traced here: 41.2 us
  Pallas kernels  40.6 us (98%)
  between operations  0.64 us (2%)
    pallas_call x1, Pallas kernels, local(): pl.pallas_call(functools.partial(kernel, nodes, locals_, shards, experts,...  38.4 us
    pallas_call x1, Pallas kernels, local(): pl.pallas_call(functools.partial(finish, experts), out_shape=(jax.ShapeDt...  2.15 us

profile of v2, /device:TPU:1, one launch (start us, length us, event | category | flops | bytes accessed | tf_op | source)
XLA Modules:
  0.0 41.2 jit_solution(2147736396428928168)
XLA Ops:
  0.6 38.4 %shard_map.95 = (bf16[2,32,8,640]{3,2,1,0:T(8,128)(2,1)}, bf16[128,256]{1,0:T(8,128)(2,1)}, f32[128,1]{1,0:T(8,128)}, f32[8,2,128]{2,1,0:T(2,128)}) custom-call(bf16[128,1280]{1,0:T(8,128)(2,1)} %tok_hbm.1, s32[1,128]{1,0:T(1,128)} %bitcast.5, s32[1,128]{1,0:T(1,128)} %bitcast.6, s32[1,128]{1,0:T(1,128)} %bitcast.7, bf16[2,1280]{1,0:T(2,128)(2,1)} %emb_hbm.1, ...), custom_call_target="tpu_custom_call" | custom-call | tf_op jit(solution)/shard_map/pallas_call | solution.py:298
  39.1 2.1 %shard_map.96 = (bf16[128,1280]{1,0:T(8,128)(2,1)}, f32[4]{0:T(128)}) custom-call(bf16[2,32,8,640]{3,2,1,0:T(8,128)(2,1)} %get-tuple-element.6.ret, bf16[128,256]{1,0:T(8,128)(2,1)} %get-tuple-element.7.pick, f32[128,1]{1,0:T(8,128)} %get-tuple-element.8.scale, f32[8,2,128]{2,1,0:T(2,128)} %get-tuple-element.9.all_stats), custom_call_target="tpu_custom_call" | custom-call | tf_op jit(solution)/shard_map/pallas_call | solution.py:349
